TPU v7x, 32 devices: a whole 2x2x4 slice. The times are simulated.
32 devices in a mesh: grp: 4 (over z), row: 4 (over y, core), col: 2 (over x).
Axes of the slice: x: 2, y: 2, z: 4, core: 2. Of those that a mesh axis runs over, the one named last changes fastest.
Arguments:
- tokens: bfloat16 [2048, 4608], P(('grp', 'row', 'col')), parts along dimension 0, may hold values from -6 to 6
- ln_gain: float32 [4608], replicated, may hold values from 0.1 to 1.9
- w_in: bfloat16 [4608, 12288], P('row', 'col'), may hold values from -0.09375 to 0.09375
- b_in: float32 [12288], P('col'), may hold values from -3 to 3
- w_out: bfloat16 [12288, 4608], P('col', 'row'), may hold values from -0.0546875 to 0.0546875
- b_out: float32 [4608], P('row'), may hold values from -3 to 3
Outputs:
- result: bfloat16 [2048, 4608], P(('grp', 'row', 'col')), parts along dimension 0
There are 4 independent parts, one for each index of `grp`. A program takes and returns all parts, laid end to end along the dimension named above; an argument that names none is the same for every part. Nothing has to cross between parts.
All inputs are finite; a program needn't handle non-finite values.
Results may differ from a plain program's by a relative error of at most 0.0095.
Values may be sent and summed in bfloat16 or wider, within the bound.
A program may use at most 128 MiB of HBM per device.

v0:
```python
import jax
import jax.numpy as jnp
from jax import lax
from jax.sharding import PartitionSpec as P


def local(tokens, ln_gain, w_in, b_in, w_out, b_out):
    values = tokens.astype(jnp.float32)
    row_mean = jnp.mean(values, axis=1, keepdims=True)
    centered = values - row_mean
    row_var = jnp.mean(centered * centered, axis=1, keepdims=True)
    normed = (centered * lax.rsqrt(row_var + 1e-06) * ln_gain).astype(jnp.bfloat16)
    own_cols = lax.all_to_all(normed, "row", split_axis=1, concat_axis=0, tiled=True)
    partial_pre = jnp.dot(
        lax.all_gather(own_cols, "col", axis=0, tiled=True),
        w_in,
        preferred_element_type=jnp.float32,
    )
    preact = lax.psum_scatter(partial_pre, "row", scatter_dimension=0, tiled=True) + b_in
    hidden = jax.nn.gelu(preact, approximate=False).astype(jnp.bfloat16)
    down_part = jnp.dot(
        lax.all_gather(hidden, "row", axis=0, tiled=True), w_out, preferred_element_type=jnp.float32
    )
    summed = lax.psum_scatter(
        down_part.astype(jnp.bfloat16), "col", scatter_dimension=0, tiled=True
    ).astype(jnp.float32)
    branch_out = (summed + b_out).astype(jnp.bfloat16)
    regrouped = lax.all_to_all(branch_out, "row", split_axis=0, concat_axis=1, tiled=True)
    return (values + regrouped.astype(jnp.float32)).astype(jnp.bfloat16)


def solution(mesh):
    in_specs = (
        P(("grp", "row", "col"), None),
        P(),
        P("row", "col"),
        P("col"),
        P("col", "row"),
        P("row"),
    )
    out_specs = P(("grp", "row", "col"), None)
    return jax.shard_map(local, mesh=mesh, in_specs=in_specs, out_specs=out_specs, check_vma=False)
```

profile of v0, /device:TPU:0, one launch (start us, length us, event | category | flops | bytes accessed | tf_op | source)
XLA Modules:
  0.0 273.9 jit_solution(3473818325535875934)
XLA Ops:
  6.5 0.0 all-gather.3.cloned.1.call-start
  6.5 1.2 convert_reduce_fusion
  7.8 1.4 fusion.12
  9.2 1.3 fusion.14
  10.6 13.7 %all_to_all.32 = bf16[64,4,1152]{2,0,1:T(8,128)(2,1)} all-to-all(bf16[64,4,1152]{2,0,1:T(8,128)(2,1)S(1)} %bitcast.19), channel_id=1, replica_groups=mesh['grp'=4,'row'=4,'col'=2] {'row'}, dimensions={1} | all-to-all | bytes 1179648 | tf_op jit(solution)/shard_map/all_to_all | solution.py:13
  24.3 0.0 all-gather.3.cloned.1.call-update
  24.3 0.0 reduce-scatter.3.cloned.1.call-start
  24.3 23.6 %all-gather.3.cloned.1.call-done = bf16[512,1152]{1,0:T(8,128)(2,1)} async-done(((bf16[256,1152]{1,0:T(8,128)(2,1)}), bf16[512,1152]{1,0:T(8,128)(2,1)}) %all-gather.3.cloned.1.call-update) | async-done | bytes 1179664 | tf_op jit(solution)/shard_map/all_gather | solution.py:15
  47.9 14.4 %fusion.16 = f32[512,6144]{1,0:T(8,128)} fusion(bf16[512,1152]{1,0:T(8,128)(2,1)} %all-gather.3.cloned.1.call-done, bf16[1152,6144]{1,0:T(8,128)(2,1)} %param.8), kind=kOutput, calls=%fused_computation.34 | convolution fusion | flops 7247757312 | bytes 27918336 | tf_op jit(solution)/shard_map/dot_general | solution.py:14
  62.3 0.0 copy-start.1
  62.3 0.0 reduce-scatter.3.cloned.1.call-update
  62.3 0.0 all-gather.5.cloned.1.call-start
  62.4 99.7 %reduce-scatter.3.cloned.1.call-done = f32[128,6144]{1,0:T(8,128)} async-done(((f32[512,6144]{1,0:T(8,128)}), f32[128,6144]{1,0:T(8,128)}) %reduce-scatter.3.cloned.1.call-update) | async-done | bytes 3145744 | tf_op jit(solution)/shard_map/reduce_scatter | solution.py:19
  162.1 0.0 copy-done.1
  162.1 8.8 %fusion.2 = bf16[128,6144]{1,0:T(8,128)(2,1)} fusion(f32[128,6144]{1,0:T(8,128)} %reduce-scatter.3.cloned.1.call-done, f32[6144]{0:T(1024)S(1)} %copy-done.1), kind=kLoop, calls=%fused_computation.3 | loop fusion | flops 51904512 | bytes 4743168 | tf_op jit(solution)/shard_map/convert_element_type | solution.py:20
  170.9 0.0 all-gather.5.cloned.1.call-update
  170.9 0.0 copy-start.2
  170.9 0.0 reduce-scatter.5.cloned.1.call-start
  171.0 46.4 %all-gather.5.cloned.1.call-done = bf16[512,6144]{1,0:T(8,128)(2,1)} async-done(((bf16[128,6144]{1,0:T(8,128)(2,1)}), bf16[512,6144]{1,0:T(8,128)(2,1)}) %all-gather.5.cloned.1.call-update) | async-done | bytes 6291472 | tf_op jit(solution)/shard_map/all_gather | solution.py:22
  217.4 13.6 %convolution_convert_fusion = bf16[512,1152]{1,0:T(8,128)(2,1)} fusion(bf16[512,6144]{1,0:T(8,128)(2,1)} %all-gather.5.cloned.1.call-done, bf16[6144,1152]{1,0:T(8,128)(2,1)} %param.10), kind=kOutput, calls=%fused_computation.19 | convolution fusion | flops 7248347136 | bytes 21626880 | tf_op jit(solution)/shard_map/dot_general | solution.py:21
  231.0 0.0 reduce-scatter.5.cloned.1.call-update
  231.0 0.0 copy-start
  231.0 22.0 %reduce-scatter.5.cloned.1.call-done = bf16[256,1152]{1,0:T(8,128)(2,1)} async-done(((bf16[512,1152]{1,0:T(8,128)(2,1)}), bf16[256,1152]{1,0:T(8,128)(2,1)}) %reduce-scatter.5.cloned.1.call-update) | async-done | bytes 589840 | tf_op jit(solution)/shard_map/reduce_scatter | solution.py:24
  253.0 0.0 copy-done.2
  253.0 1.2 add_convert_fusion
  254.1 12.1 %all_to_all.33 = bf16[4,64,1152]{2,1,0:T(8,128)(2,1)S(1)} all-to-all(bf16[4,64,1152]{2,1,0:T(8,128)(2,1)S(1)} %bitcast.20), channel_id=1, replica_groups=mesh['grp'=4,'row'=4,'col'=2] {'row'}, dimensions={0} | all-to-all | bytes 1179648 | tf_op jit(solution)/shard_map/all_to_all | solution.py:28
  266.2 0.1 convert_bitcast_fusion
  266.3 0.1 copy.14
  266.4 0.0 copy-done
  266.4 0.9 fusion.15
  (3 shorter events, 0.1 us)
Async XLA Ops:
  6.5 41.3 %all-gather.3.cloned.1.call-start = ((), (), s32[]{:S(2)}) async-start(), calls=%async_computation.4 | async-start | bytes 1769472 | tf_op jit(solution)/shard_map/all_gather | solution.py:15
  24.3 137.8 %reduce-scatter.3.cloned.1.call-start = ((), (), s32[]{:S(2)}) async-start(), calls=%async_computation.5 | async-start | bytes 15728640 | tf_op jit(solution)/shard_map/reduce_scatter | solution.py:19
  62.3 99.8 %copy-start.1 = (f32[6144]{0:T(1024)S(1)}, f32[6144]{0:T(1024)}, u32[]{:S(2)}) copy-start(f32[6144]{0:T(1024)} %param.9) | copy-start | bytes 73732
  62.3 155.1 %all-gather.5.cloned.1.call-start = ((), (), s32[]{:S(2)}) async-start(), calls=%async_computation.6 | async-start | bytes 7864320 | tf_op jit(solution)/shard_map/all_gather | solution.py:22
  170.9 82.1 %copy-start.2 = (f32[1152]{0:T(1024)S(1)}, f32[1152]{0:T(1024)}, u32[]{:S(2)}) copy-start(f32[1152]{0:T(1024)} %param.11) | copy-start | bytes 13828
  170.9 82.0 %reduce-scatter.5.cloned.1.call-start = ((), (), s32[]{:S(2)}) async-start(), calls=%async_computation.7 | async-start | bytes 1769472 | tf_op jit(solution)/shard_map/reduce_scatter | solution.py:24
  231.0 35.4 %copy-start = (bf16[64,4608]{1,0:T(8,128)(2,1)S(1)}, bf16[64,4608]{1,0:T(8,128)(2,1)}, u32[]{:S(2)}) copy-start(bf16[64,4608]{1,0:T(8,128)(2,1)} %param.6) | copy-start | bytes 1769476
Sparse Core Ops, SparseCore 0:
  24.4 23.4 all-gather.2
  62.5 99.6 reduce-scatter.2
  171.0 46.3 all-gather.4
  231.1 21.8 reduce-scatter.4
where the time goes:
time: 274 us
  waiting for transfers between devices  192 us (70%)
  matrix products  28 us (10%)
  blocking collectives  25.8 us (9%)
  other arithmetic  14.9 us (5%)
  between operations  13.2 us (5%)
    reduce_scatter x1, waiting for transfers between devices, local(): lax.psum_scatter(partial_pre, 'row', scatter_dimension=0, tiled=True) + b_in  99.7 us
    all_gather x1, waiting for transfers between devices, local(): lax.all_gather(hidden, 'row', axis=0, tiled=True)  46.4 us
    all_gather x1, waiting for transfers between devices, local(): lax.all_gather(own_cols, 'col', axis=0, tiled=True)  23.6 us
    reduce_scatter x1, waiting for transfers between devices, local(): lax.psum_scatter(down_part.astype(jnp.bfloat16), 'col', scatter_dimension...  22 us
    dot_general x1, matrix products, local(): jnp.dot(lax.all_gather(own_cols, 'col', axis=0, tiled=True), w_in, prefer...  14.4 us
    all_to_all x1, blocking collectives, local(): lax.all_to_all(normed, 'row', split_axis=1, concat_axis=0, tiled=True)  13.7 us
    dot_general x1, matrix products, local(): jnp.dot(lax.all_gather(hidden, 'row', axis=0, tiled=True), w_out, preferr...  13.6 us
    all_to_all x1, blocking collectives, local(): lax.all_to_all(branch_out, 'row', split_axis=0, concat_axis=1, tiled=True)  12.1 us
  transfers between devices with their start and end apart: 4, of which 4 were waited for; matrix products, arithmetic and copies ran while one was open for 0% of the time, Pallas kernels for 0%

commit v1 on v0

--- a/solution.py
+++ b/solution.py
@@ -1,7 +1,269 @@
+import functools
+
 import jax
 import jax.numpy as jnp
 from jax import lax
+from jax.experimental import pallas as pl
+from jax.experimental.pallas import tpu as pltpu
 from jax.sharding import PartitionSpec as P
+
+MESH = pl.DeviceIdType.MESH
+F32, BF16 = jnp.float32, jnp.bfloat16
+CHUNKS = 4
+
+
+def tile_of(size, limit):
+    return next(t for t in range(limit, 0, -128) if size % t == 0)
+
+
+def block_kernel(
+    tokens_ref, gain_ref, w_in_hbm, b_in_ref, w_out_hbm, b_out_ref, out_ref,
+    w_in, w_out, normed, panel, mine, psend, precv, ssend, srecv, hidden, okeep, osend, orecv, branch, regrouped,
+    w_sem, in_send, in_recv, fwd_send, fwd_recv, p_sem, s_sem, h_sem, o_sem, b_send, b_recv,
+):
+    r, c = lax.axis_index("row"), lax.axis_index("col")
+    y, k = r // 2, r % 2
+    partner, across = 2 * y + (1 - k), 2 * (1 - y) + k
+    rows, width = tokens_ref.shape
+    quarter = width // 4
+    half = mine.shape[1]
+    depth = w_in.shape[0]
+
+    def remote(src, dst, send, recv, row, col=None):
+        target = {"row": row} if col is None else {"row": row, "col": col}
+        return pltpu.make_async_remote_copy(
+            src_ref=src, dst_ref=dst, send_sem=send, recv_sem=recv, device_id=target, device_id_type=MESH
+        )
+
+    w_copies = []
+    for which, (src, dst) in enumerate(((w_in_hbm, w_in), (w_out_hbm, w_out))):
+        step = src.shape[0] // 4
+        for part in range(4):
+            cut = pl.ds(part * step, step)
+            copy = pltpu.make_async_copy(src.at[cut], dst.at[cut], w_sem.at[which, part])
+            copy.start()
+            w_copies.append(copy)
+
+    barrier = pltpu.get_barrier_semaphore()
+    for target in ({"row": (r + 1) % 4}, {"row": (r + 2) % 4}, {"row": (r + 3) % 4}, {"col": 1 - c}):
+        pl.semaphore_signal(barrier, inc=1, device_id=target, device_id_type=MESH)
+
+    group = 16
+
+    @pl.loop(0, rows // group)
+    def _(i):
+        at = pl.ds(pl.multiple_of(i * group, group), group)
+        values = tokens_ref[at, :].astype(F32)
+        centered = values - jnp.mean(values, axis=1, keepdims=True)
+        var = jnp.mean(centered * centered, axis=1, keepdims=True)
+        scaled = (centered * lax.rsqrt(var + 1e-06) * gain_ref[...]).astype(BF16)
+        for q in range(4):
+            normed[q, at, :] = scaled[:, q * quarter : (q + 1) * quarter]
+
+    panel[k, y] = normed[r]
+    pl.semaphore_wait(barrier, 4)
+
+    def piece(d):
+        to = (r + d) % 4
+        return remote(normed.at[to], panel.at[k, y], in_send.at[d - 1], in_recv.at[k, y], to)
+
+    for d in (1, 2, 3):
+        piece(d).start()
+
+    def forward(kk, yy):
+        return remote(
+            panel.at[kk, yy], panel.at[2 + kk, yy], fwd_send.at[kk, yy], fwd_recv.at[kk, yy], r, 1 - c
+        )
+
+    tile = tile_of(half, 512)
+    tiles = half // tile
+
+    def share(j):
+        return remote(psend.at[j], precv.at[j], p_sem.at[0, j], p_sem.at[1, j], partner)
+
+    def cross(j):
+        return remote(ssend.at[j], srecv.at[j], s_sem.at[0, j], s_sem.at[1, j], across)
+
+    def spread(j):
+        return remote(hidden.at[j, k], hidden.at[j, k], h_sem.at[0, j], h_sem.at[1, j], partner)
+
+    def lend(j):
+        return remote(osend.at[j], orecv.at[j], o_sem.at[0, j], o_sem.at[1, j], r, 1 - c)
+
+    def give(j, yy):
+        return remote(branch.at[j, yy], regrouped.at[r], b_send.at[j, yy], b_recv.at[r], 2 * yy + j)
+
+    def first(j):
+        for yy in range(2):
+            if j < 2:
+
+                @pl.when(jnp.logical_or(k != j, y != yy))
+                def _():
+                    remote(panel.at[j, yy], panel.at[j, yy], in_send.at[0], in_recv.at[j, yy], across).wait_recv()
+
+                forward(j, yy).start()
+            else:
+                forward(j - 2, yy).wait_recv()
+        if j == 0:
+            for copy in w_copies[:4]:
+                copy.wait()
+
+        @pl.loop(0, tiles)
+        def _(t):
+            here = pl.ds(pl.multiple_of(t * tile, tile), tile)
+            there = pl.ds(pl.multiple_of((1 - k) * half + t * tile, tile), tile)
+            x = panel[j].reshape(2 * rows, depth)
+            psend[j, :, here] = jnp.dot(x, w_in[:, there], preferred_element_type=F32).astype(BF16)
+
+        share(j).start()
+
+        @pl.loop(0, tiles)
+        def _(t):
+            here = pl.ds(pl.multiple_of(t * tile, tile), tile)
+            own = pl.ds(pl.multiple_of(k * half + t * tile, tile), tile)
+            x = panel[j].reshape(2 * rows, depth)
+            mine[:, here] = jnp.dot(x, w_in[:, own], preferred_element_type=F32)
+
+        share(j).wait_recv()
+
+        @pl.loop(0, tiles)
+        def _(t):
+            here = pl.ds(pl.multiple_of(t * tile, tile), tile)
+            ssend[j, :, here] = (mine[:, here] + precv[j, :, here].astype(F32)).astype(BF16)
+
+        cross(j).start()
+
+    def second(j):
+        cross(j).wait_recv()
+
+        @pl.loop(0, tiles)
+        def _(t):
+            here = pl.ds(pl.multiple_of(t * tile, tile), tile)
+            v = ssend[j, :, here].astype(F32) + srecv[j, :, here].astype(F32) + b_in_ref[pl.ds(k, 1), here]
+            hidden[j, k, :, here] = (v * (1.0 + lax.erf(v * (0.5**0.5))) * 0.5).astype(BF16)
+
+        spread(j).start()
+        if j == 0:
+            for copy in w_copies[4:]:
+                copy.wait()
+        total = okeep.at[j] if j < 2 else okeep.at[2]
+
+        def down(which, t):
+            here = pl.ds(pl.multiple_of(t * tile, tile), tile)
+            deep = pl.ds(pl.multiple_of(which * half + t * tile, tile), tile)
+            return jnp.dot(hidden[j, which, :, here], w_out[deep, :], preferred_element_type=F32)
+
+        total[...] = down(k, 0)
+
+        @pl.loop(1, tiles)
+        def _(t):
+            total[...] += down(k, t)
+
+        remote(
+            hidden.at[j, 1 - k], hidden.at[j, 1 - k], h_sem.at[0, j], h_sem.at[1, j], partner
+        ).wait_recv()
+
+        @pl.loop(0, tiles)
+        def _(t):
+            total[...] += down(1 - k, t)
+
+        if j >= 2:
+            osend[j - 2] = total[...].astype(BF16)
+            lend(j - 2).start()
+
+    def finish(j):
+        lend(j).wait_recv()
+        summed = okeep[j] + orecv[j].astype(F32) + b_out_ref[...]
+        branch[j] = summed.astype(BF16).reshape(2, rows, quarter)
+        for yy in range(2):
+            own = jnp.logical_and(k == j, y == yy)
+
+            @pl.when(own)
+            def _():
+                regrouped[r] = branch[j, yy]
+
+            @pl.when(jnp.logical_not(own))
+            def _():
+                give(j, yy).start()
+
+    for j in range(CHUNKS):
+        first(j)
+    for j in range(CHUNKS):
+        second(j)
+    for j in range(2):
+        finish(j)
+
+    for q in range(4):
+
+        @pl.when(r != q)
+        def _():
+            remote(regrouped.at[q], regrouped.at[q], b_send.at[0, 0], b_recv.at[q], across).wait_recv()
+
+        cut = pl.ds(q * quarter, quarter)
+        out_ref[:, cut] = (tokens_ref[:, cut].astype(F32) + regrouped[q].astype(F32)).astype(BF16)
+
+    for d in (1, 2, 3):
+        piece(d).wait_send()
+    for kk in range(2):
+        for yy in range(2):
+            forward(kk, yy).wait_send()
+    for j in range(CHUNKS):
+        share(j).wait_send()
+        cross(j).wait_send()
+        spread(j).wait_send()
+    for j in range(2):
+        lend(j).wait_send()
+        for yy in range(2):
+
+            @pl.when(jnp.logical_or(k != j, y != yy))
+            def _():
+                give(j, yy).wait_send()
+
+
+def fused(tokens, ln_gain, w_in, b_in, w_out, b_out):
+    rows, width = tokens.shape
+    depth, units = w_in.shape
+    half, chunk = units // 2, 2 * rows
+    vmem, dma = pltpu.VMEM, pltpu.SemaphoreType.DMA
+    in_vmem, in_hbm = pl.BlockSpec(memory_space=vmem), pl.BlockSpec(memory_space=pl.ANY)
+    return pl.pallas_call(
+        block_kernel,
+        out_shape=jax.ShapeDtypeStruct((rows, width), BF16),
+        in_specs=[in_vmem, in_vmem, in_hbm, in_vmem, in_hbm, in_vmem],
+        out_specs=in_vmem,
+        scratch_shapes=[
+            vmem(w_in.shape, BF16),
+            vmem(w_out.shape, BF16),
+            vmem((4, rows, depth), BF16),
+            vmem((CHUNKS, 2, rows, depth), BF16),
+            vmem((chunk, half), F32),
+            vmem((CHUNKS, chunk, half), BF16),
+            vmem((CHUNKS, chunk, half), BF16),
+            vmem((CHUNKS, chunk, half), BF16),
+            vmem((CHUNKS, chunk, half), BF16),
+            vmem((CHUNKS, 2, chunk, half), BF16),
+            vmem((3, chunk, depth), F32),
+            vmem((2, chunk, depth), BF16),
+            vmem((2, chunk, depth), BF16),
+            vmem((2, 2, rows, depth), BF16),
+            vmem((4, rows, depth), BF16),
+            dma((2, 4)),
+            dma((3,)),
+            dma((2, 2)),
+            dma((2, 2)),
+            dma((2, 2)),
+            dma((2, CHUNKS)),
+            dma((2, CHUNKS)),
+            dma((2, CHUNKS)),
+            dma((2, 2)),
+            dma((2, 2)),
+            dma((4,)),
+        ],
+        compiler_params=pltpu.CompilerParams(
+            collective_id=0, has_side_effects=True, vmem_limit_bytes=67043328
+        ),
+        name="mlp_block",
+    )(tokens, ln_gain.reshape(1, -1), w_in, b_in.reshape(2, -1), w_out, b_out.reshape(1, -1))
 
 
 def local(tokens, ln_gain, w_in, b_in, w_out, b_out):
@@ -39,4 +301,5 @@
         P("row"),
     )
     out_specs = P(("grp", "row", "col"), None)
-    return jax.shard_map(local, mesh=mesh, in_specs=in_specs, out_specs=out_specs, check_vma=False)
+    body = fused if (mesh.shape["row"], mesh.shape["col"]) == (4, 2) else local
+    return jax.shard_map(body, mesh=mesh, in_specs=in_specs, out_specs=out_specs, check_vma=False)

time: 274 us -> 111 us (0.41)
  waiting for transfers between devices: 192 us -> 0 us
  Pallas kernels: 0 us -> 104 us
  matrix products: 28 us -> 0 us
  blocking collectives: 25.8 us -> 0 us
  other arithmetic: 14.9 us -> 0 us
  between operations: 13.2 us -> 0.01 us
  local copies, waits for them, and re-layouts: 0.15 us -> 5.89 us
    reduce_scatter x2 -> x0, waiting for transfers between devices: 122 us -> none  [the longest x1 99.7 us: local(): lax.psum_scatter(partial_pre, 'row', scatter_dimension=0, tiled=True) + b_in]
    pallas_call x0 -> x1, Pallas kernels: none -> 104 us  [fused(): pl.pallas_call(block_kernel, out_shape=jax.ShapeDtypeStruct((rows, width)...]
    all_gather x2 -> x0, waiting for transfers between devices: 70 us -> none  [the longest x1 46.4 us: local(): lax.all_gather(hidden, 'row', axis=0, tiled=True)]
    dot_general x2 -> x0, matrix products: 28 us -> none  [the longest x1 14.4 us: local(): jnp.dot(lax.all_gather(own_cols, 'col', axis=0, tiled=True), w_in, prefer...]
    all_to_all x2 -> x0, blocking collectives: 25.8 us -> none  [the longest x1 13.7 us: local(): lax.all_to_all(normed, 'row', split_axis=1, concat_axis=0, tiled=True)]
    convert_element_type x4 -> x0, other arithmetic: 12.2 us -> none  [the longest x1 8.79 us: local(): hidden = jax.nn.gelu(preact, approximate=False).astype(jnp.bfloat16)]
    reshape x0 -> x3, local copies, waits for them, and re-layouts: none -> 3.97 us  [the longest x1 1.36 us: fused(): b_in.reshape(2, -1)]
  transfers between devices with their start and end apart: 4 -> 0, of which waited for: 4 -> 0; matrix products, arithmetic and copies ran while one was open for 0% -> 0% of each run, Pallas kernels for 0% -> 0%
where the time goes in v1:
time: 111 us; the launch traced here: 110 us
  Pallas kernels  104 us (94%)
  local copies, waits for them, and re-layouts  5.89 us (5%)
    pallas_call x1, Pallas kernels, fused(): pl.pallas_call(block_kernel, out_shape=jax.ShapeDtypeStruct((rows, width)...  104 us

profile of v1, /device:TPU:0, one launch (start us, length us, event | category | flops | bytes accessed | tf_op | source)
XLA Modules:
  0.0 110.3 jit_solution(8998494306695073469)
XLA Ops:
  0.0 1.3 %reshape.11.b_out_ref = f32[1,1152]{1,0:T(1,128)} reshape(f32[1152]{0:T(1024)} %param.11) | data formatting | bytes 9216 | tf_op jit(solution)/shard_map/reshape | solution.py:266
  1.3 1.3 %reshape.9.gain_ref = f32[1,4608]{1,0:T(1,128)} reshape(f32[4608]{0:T(1024)} %param.7) | data formatting | bytes 36864 | tf_op jit(solution)/shard_map/reshape | solution.py:266
  2.6 1.4 %reshape.10.b_in_ref = f32[2,3072]{1,0:T(2,128)} reshape(f32[6144]{0:T(1024)} %param.9) | data formatting | bytes 49152 | tf_op jit(solution)/shard_map/reshape | solution.py:266
  4.0 104.4 %mlp_block.1 = bf16[64,4608]{1,0:T(8,128)(2,1)} custom-call(bf16[64,4608]{1,0:T(8,128)(2,1)} %tokens_ref.1, f32[1,4608]{1,0:T(1,128)} %reshape.9.gain_ref, bf16[1152,6144]{1,0:T(8,128)(2,1)} %w_in_hbm.1, f32[2,3072]{1,0:T(2,128)} %reshape.10.b_in_ref, bf16[6144,1152]{1,0:T(8,128)(2,1)} %w_out_hbm.1, f32[1,1152]{1,0:T(1,128)} %reshape.11.b_out_ref), custom_call_target="tpu_custom_call" | custom-call | tf_op jit(solution)/shard_map/mlp_block/pallas_call | solution.py:229
  108.4 1.9 %copy.8 = bf16[64,4608]{1,0:T(8,128)(2,1)} copy(bf16[64,4608]{1,0:T(8,128)(2,1)} %mlp_block.1) | data formatting | bytes 1179648

commit v2 on v0

--- a/solution.py
+++ b/solution.py
@@ -1,7 +1,317 @@
+import functools
+
 import jax
 import jax.numpy as jnp
 from jax import lax
+from jax.experimental import pallas as pl
+from jax.experimental.pallas import tpu as pltpu
 from jax.sharding import PartitionSpec as P
+
+MESH = pl.DeviceIdType.MESH
+F32, BF16 = jnp.float32, jnp.bfloat16
+
+
+def ranges(rows):
+    q = rows // 4
+    return [(0, 0, q), (0, q, 2 * q), (0, 2 * q, rows), (1, 0, 2 * q), (1, 2 * q, 3 * q), (1, 3 * q, rows)]
+
+
+def tile_of(size, limit):
+    return next(t for t in range(limit, 0, -128) if size % t == 0)
+
+
+def block_kernel(
+    tokens_ref, gain_ref, w_in_hbm, b_in_ref, w_out_hbm, b_out_ref, out_ref,
+    w_in, w_out, normed, panel, mine, psend, precv, ssend, srecv, hidden, total, okeep, osend, orecv, branch, regrouped,
+    w_sem, in_send, in_recv, fwd_sem, p_sem, s_sem, h_sem, o_sem, b_send, b_recv,
+):
+    r, c = lax.axis_index("row"), lax.axis_index("col")
+    y, k = r // 2, r % 2
+    partner, across = 2 * y + (1 - k), 2 * (1 - y) + k
+    rows, width = tokens_ref.shape
+    quarter = width // 4
+    half = mine.shape[1]
+    depth = w_in.shape[0]
+    chunks = ranges(rows)
+    own = [j for j, chunk in enumerate(chunks) if chunk[0] == 0]
+    other = [j for j, chunk in enumerate(chunks) if chunk[0] == 1]
+
+    def span(j):
+        _, lo, hi = chunks[j]
+        return pl.ds(lo, hi - lo)
+
+    def flat(j):
+        cc, lo, hi = chunks[j]
+        return pl.ds(4 * (cc * rows + lo), 4 * (hi - lo))
+
+    def remote(src, dst, send, recv, row, col=None):
+        target = {"row": row} if col is None else {"row": row, "col": col}
+        return pltpu.make_async_remote_copy(
+            src_ref=src, dst_ref=dst, send_sem=send, recv_sem=recv, device_id=target, device_id_type=MESH
+        )
+
+    def load(which, part):
+        src, dst = ((w_in_hbm, w_in), (w_out_hbm, w_out))[which]
+        step = src.shape[0] // 4
+        cut = pl.ds(part * step, step)
+        return pltpu.make_async_copy(src.at[cut], dst.at[cut], w_sem.at[which, part])
+
+    for part in range(4):
+        load(0, part).start()
+
+    barrier = pltpu.get_barrier_semaphore()
+    for target in ({"row": (r + 1) % 4}, {"row": (r + 2) % 4}, {"row": (r + 3) % 4}, {"col": 1 - c}):
+        pl.semaphore_signal(barrier, inc=1, device_id=target, device_id_type=MESH)
+
+    def normalize(j):
+        _, lo, hi = chunks[j]
+        for start in range(lo, hi, rows // 4):
+            at = pl.ds(start, rows // 4)
+            values = tokens_ref[at, :].astype(F32)
+            centered = values - jnp.mean(values, axis=1, keepdims=True)
+            var = jnp.mean(centered * centered, axis=1, keepdims=True)
+            scaled = (centered * lax.rsqrt(var + 1e-06) * gain_ref[...]).astype(BF16)
+            for q in range(4):
+                normed[q, at, :] = scaled[:, q * quarter : (q + 1) * quarter]
+        panel[0, r, span(j), :] = normed[r, span(j), :]
+
+    def piece(j, d):
+        to = (r + d) % 4
+        return remote(
+            normed.at[to, span(j)], panel.at[0, r, span(j)], in_send.at[j, d - 1], in_recv.at[j, r], to
+        )
+
+    for j in own:
+        normalize(j)
+        if j == 0:
+            pl.semaphore_wait(barrier, 4)
+        for d in (1, 2, 3):
+            piece(j, d).start()
+
+    def forward(j):
+        return remote(
+            panel.at[0, :, span(j)], panel.at[1, :, span(j)], fwd_sem.at[0, j], fwd_sem.at[1, j], r, 1 - c
+        )
+
+    tile = tile_of(half, 512)
+    tiles = half // tile
+
+    def share(j):
+        return remote(psend.at[flat(j)], precv.at[flat(j)], p_sem.at[0, j], p_sem.at[1, j], partner)
+
+    def cross(j):
+        return remote(ssend.at[flat(j)], srecv.at[flat(j)], s_sem.at[0, j], s_sem.at[1, j], across)
+
+    def spread(j, which):
+        held = hidden.at[which, flat(j)]
+        return remote(held, held, h_sem.at[0, j], h_sem.at[1, j], partner)
+
+    def lend(j):
+        i = j - len(own)
+        return remote(osend.at[:, span(j)], orecv.at[:, span(j)], o_sem.at[0, i], o_sem.at[1, i], r, 1 - c)
+
+    def give(j, q):
+        i = j - len(own)
+        return remote(
+            branch.at[q, span(j)], regrouped.at[r, span(j)], b_send.at[i, q], b_recv.at[i, r], q
+        )
+
+    forwarded = []
+
+    def first(j):
+        cc, lo, hi = chunks[j]
+        count = 4 * (hi - lo)
+        if cc == 0:
+            for q in range(4):
+
+                @pl.when(r != q)
+                def _():
+                    held = panel.at[0, q, span(j)]
+                    remote(held, held, in_send.at[j, 0], in_recv.at[j, q], across).wait_recv()
+
+            forward(j).start()
+        else:
+            for i in own:
+                if i not in forwarded and chunks[i][1] < hi:
+                    forward(i).wait_recv()
+                    forwarded.append(i)
+        if j == 0:
+            for part in range(4):
+                load(0, part).wait()
+            for part in range(4):
+                load(1, part).start()
+
+        @pl.loop(0, tiles)
+        def _(t):
+            here = pl.ds(pl.multiple_of(t * tile, tile), tile)
+            there = pl.ds(pl.multiple_of((1 - k) * half + t * tile, tile), tile)
+            x = panel[cc, :, span(j), :].reshape(count, depth)
+            psend[flat(j), here] = jnp.dot(x, w_in[:, there], preferred_element_type=F32).astype(BF16)
+
+        share(j).start()
+
+        @pl.loop(0, tiles)
+        def _(t):
+            here = pl.ds(pl.multiple_of(t * tile, tile), tile)
+            mine_at = pl.ds(pl.multiple_of(k * half + t * tile, tile), tile)
+            x = panel[cc, :, span(j), :].reshape(count, depth)
+            mine[pl.ds(0, count), here] = jnp.dot(x, w_in[:, mine_at], preferred_element_type=F32)
+
+        share(j).wait_recv()
+
+        @pl.loop(0, tiles)
+        def _(t):
+            here = pl.ds(pl.multiple_of(t * tile, tile), tile)
+            ssend[flat(j), here] = (mine[pl.ds(0, count), here] + precv[flat(j), here].astype(F32)).astype(BF16)
+
+        cross(j).start()
+
+    def second(j):
+        cc, lo, hi = chunks[j]
+        count = 4 * (hi - lo)
+        cross(j).wait_recv()
+
+        @pl.loop(0, tiles)
+        def _(t):
+            here = pl.ds(pl.multiple_of(t * tile, tile), tile)
+            v = ssend[flat(j), here].astype(F32) + srecv[flat(j), here].astype(F32) + b_in_ref[pl.ds(k, 1), here]
+            hidden[k, flat(j), here] = (v * (1.0 + lax.erf(v * (0.5**0.5))) * 0.5).astype(BF16)
+
+        spread(j, k).start()
+        if j == 0:
+            for part in range(4):
+                load(1, part).wait()
+        acc = total.at[pl.ds(0, count)]
+
+        def down(which, t):
+            here = pl.ds(pl.multiple_of(t * tile, tile), tile)
+            deep = pl.ds(pl.multiple_of(which * half + t * tile, tile), tile)
+            return jnp.dot(hidden[which, flat(j), here], w_out[deep, :], preferred_element_type=F32)
+
+        acc[...] = down(k, 0)
+
+        @pl.loop(1, tiles)
+        def _(t):
+            acc[...] += down(k, t)
+
+        spread(j, 1 - k).wait_recv()
+
+        @pl.loop(0, tiles)
+        def _(t):
+            acc[...] += down(1 - k, t)
+
+        if cc == 0:
+            okeep[:, span(j), :] = acc[...].reshape(4, hi - lo, quarter)
+        else:
+            osend[:, span(j), :] = acc[...].astype(BF16).reshape(4, hi - lo, quarter)
+            lend(j).start()
+
+    def finish(j):
+        lend(j).wait_recv()
+        for q in range(4):
+            summed = okeep[q, span(j), :] + orecv[q, span(j), :].astype(F32) + b_out_ref[...]
+            branch[q, span(j), :] = summed.astype(BF16)
+        for q in range(4):
+
+            @pl.when(r == q)
+            def _():
+                regrouped[r, span(j), :] = branch[q, span(j), :]
+
+            @pl.when(r != q)
+            def _():
+                give(j, q).start()
+
+    def settle(j):
+        i = j - len(own)
+        for q in range(4):
+
+            @pl.when(r != q)
+            def _():
+                held = regrouped.at[q, span(j)]
+                remote(held, held, b_send.at[i, 0], b_recv.at[i, q], across).wait_recv()
+
+            cut = pl.ds(q * quarter, quarter)
+            out_ref[span(j), cut] = (
+                tokens_ref[span(j), cut].astype(F32) + regrouped[q, span(j), :].astype(F32)
+            ).astype(BF16)
+
+    for j in range(len(chunks)):
+        first(j)
+    for j in range(len(chunks)):
+        second(j)
+        if j > len(own):
+            finish(j - 1)
+    for j in other[:-2]:
+        settle(j)
+    finish(other[-1])
+    for j in other[-2:]:
+        settle(j)
+
+    for j in own:
+        for d in (1, 2, 3):
+            piece(j, d).wait_send()
+        forward(j).wait_send()
+    for j in range(len(chunks)):
+        share(j).wait_send()
+        cross(j).wait_send()
+        spread(j, k).wait_send()
+    for j in other:
+        lend(j).wait_send()
+        for q in range(4):
+
+            @pl.when(r != q)
+            def _():
+                give(j, q).wait_send()
+
+
+def fused(tokens, ln_gain, w_in, b_in, w_out, b_out):
+    rows, width = tokens.shape
+    depth, units = w_in.shape
+    half = units // 2
+    chunks = ranges(rows)
+    steps = len(chunks)
+    kept = sum(chunk[0] == 0 for chunk in chunks)
+    most = 4 * max(hi - lo for _, lo, hi in chunks)
+    vmem, dma = pltpu.VMEM, pltpu.SemaphoreType.DMA
+    in_vmem, in_hbm = pl.BlockSpec(memory_space=vmem), pl.BlockSpec(memory_space=pl.ANY)
+    return pl.pallas_call(
+        block_kernel,
+        out_shape=jax.ShapeDtypeStruct((rows, width), BF16),
+        in_specs=[in_vmem, in_vmem, in_hbm, in_vmem, in_hbm, in_vmem],
+        out_specs=in_vmem,
+        scratch_shapes=[
+            vmem(w_in.shape, BF16),
+            vmem(w_out.shape, BF16),
+            vmem((4, rows, depth), BF16),
+            vmem((2, 4, rows, depth), BF16),
+            vmem((most, half), F32),
+            vmem((8 * rows, half), BF16),
+            vmem((8 * rows, half), BF16),
+            vmem((8 * rows, half), BF16),
+            vmem((8 * rows, half), BF16),
+            vmem((2, 8 * rows, half), BF16),
+            vmem((most, depth), F32),
+            vmem((4, rows, depth), F32),
+            vmem((4, rows, depth), BF16),
+            vmem((4, rows, depth), BF16),
+            vmem((4, rows, depth), BF16),
+            vmem((4, rows, depth), BF16),
+            dma((2, 4)),
+            dma((kept, 3)),
+            dma((kept, 4)),
+            dma((2, kept)),
+            dma((2, steps)),
+            dma((2, steps)),
+            dma((2, steps)),
+            dma((2, steps - kept)),
+            dma((steps - kept, 4)),
+            dma((steps - kept, 4)),
+        ],
+        compiler_params=pltpu.CompilerParams(
+            collective_id=0, has_side_effects=True, vmem_limit_bytes=67043328
+        ),
+        name="mlp_block",
+    )(tokens, ln_gain.reshape(1, -1), w_in, b_in.reshape(2, -1), w_out, b_out.reshape(1, -1))
 
 
 def local(tokens, ln_gain, w_in, b_in, w_out, b_out):
@@ -39,4 +349,5 @@
         P("row"),
     )
     out_specs = P(("grp", "row", "col"), None)
-    return jax.shard_map(local, mesh=mesh, in_specs=in_specs, out_specs=out_specs, check_vma=False)
+    body = fused if (mesh.shape["row"], mesh.shape["col"]) == (4, 2) else local
+    return jax.shard_map(body, mesh=mesh, in_specs=in_specs, out_specs=out_specs, check_vma=False)

time: 274 us -> 102 us (0.37)
  waiting for transfers between devices: 192 us -> 0 us
  Pallas kernels: 0 us -> 96 us
  matrix products: 28 us -> 0 us
  blocking collectives: 25.8 us -> 0 us
  other arithmetic: 14.9 us -> 0 us
  between operations: 13.2 us -> 0.01 us
  local copies, waits for them, and re-layouts: 0.15 us -> 5.89 us
    reduce_scatter x2 -> x0, waiting for transfers between devices: 122 us -> none  [the longest x1 99.7 us: local(): lax.psum_scatter(partial_pre, 'row', scatter_dimension=0, tiled=True) + b_in]
    pallas_call x0 -> x1, Pallas kernels: none -> 96 us  [fused(): pl.pallas_call(block_kernel, out_shape=jax.ShapeDtypeStruct((rows, width)...]
    all_gather x2 -> x0, waiting for transfers between devices: 70 us -> none  [the longest x1 46.4 us: local(): lax.all_gather(hidden, 'row', axis=0, tiled=True)]
    dot_general x2 -> x0, matrix products: 28 us -> none  [the longest x1 14.4 us: local(): jnp.dot(lax.all_gather(own_cols, 'col', axis=0, tiled=True), w_in, prefer...]
    all_to_all x2 -> x0, blocking collectives: 25.8 us -> none  [the longest x1 13.7 us: local(): lax.all_to_all(normed, 'row', split_axis=1, concat_axis=0, tiled=True)]
    convert_element_type x4 -> x0, other arithmetic: 12.2 us -> none  [the longest x1 8.79 us: local(): hidden = jax.nn.gelu(preact, approximate=False).astype(jnp.bfloat16)]
    reshape x0 -> x3, local copies, waits for them, and re-layouts: none -> 3.97 us  [the longest x1 1.36 us: fused(): b_in.reshape(2, -1)]
  transfers between devices with their start and end apart: 4 -> 0, of which waited for: 4 -> 0; matrix products, arithmetic and copies ran while one was open for 0% -> 0% of each run, Pallas kernels for 0% -> 0%
where the time goes in v2:
time: 102 us
  Pallas kernels  96 us (94%)
  local copies, waits for them, and re-layouts  5.89 us (6%)
    pallas_call x1, Pallas kernels, fused(): pl.pallas_call(block_kernel, out_shape=jax.ShapeDtypeStruct((rows, width)...  96 us

profile of v2, /device:TPU:0, one launch (start us, length us, event | category | flops | bytes accessed | tf_op | source)
XLA Modules:
  0.0 101.9 jit_solution(14974626817247706240)
XLA Ops:
  0.0 1.3 %reshape.11.b_out_ref = f32[1,1152]{1,0:T(1,128)} reshape(f32[1152]{0:T(1024)} %param.11) | data formatting | bytes 9216 | tf_op jit(solution)/shard_map/reshape | solution.py:314
  1.3 1.3 %reshape.9.gain_ref = f32[1,4608]{1,0:T(1,128)} reshape(f32[4608]{0:T(1024)} %param.7) | data formatting | bytes 36864 | tf_op jit(solution)/shard_map/reshape | solution.py:314
  2.6 1.4 %reshape.10.b_in_ref = f32[2,3072]{1,0:T(2,128)} reshape(f32[6144]{0:T(1024)} %param.9) | data formatting | bytes 49152 | tf_op jit(solution)/shard_map/reshape | solution.py:314
  4.0 96.0 %mlp_block.1 = bf16[64,4608]{1,0:T(8,128)(2,1)} custom-call(bf16[64,4608]{1,0:T(8,128)(2,1)} %tokens_ref.1, f32[1,4608]{1,0:T(1,128)} %reshape.9.gain_ref, bf16[1152,6144]{1,0:T(8,128)(2,1)} %w_in_hbm.1, f32[2,3072]{1,0:T(2,128)} %reshape.10.b_in_ref, bf16[6144,1152]{1,0:T(8,128)(2,1)} %w_out_hbm.1, f32[1,1152]{1,0:T(1,128)} %reshape.11.b_out_ref), custom_call_target="tpu_custom_call" | custom-call | tf_op jit(solution)/shard_map/mlp_block/pallas_call | solution.py:277
  99.9 1.9 %copy.8 = bf16[64,4608]{1,0:T(8,128)(2,1)} copy(bf16[64,4608]{1,0:T(8,128)(2,1)} %mlp_block.1) | data formatting | bytes 1179648
